TPU v7x, 512 devices: a whole 4x4x16 slice. The times are simulated.
512 devices in a mesh: row: 32 (over z, core), vec: 16 (over y, x).
Axes of the slice: x: 4, y: 4, z: 16, core: 2. Of those that a mesh axis runs over, the one named last changes fastest.
Arguments:
- vectors: float32 [32768, 2048], P('row', 'vec'), may hold values from -6 to 6
- reflectors: float32 [3, 32768, 512], P(None, ('row', 'vec')), may hold values from -0.03125 to 0.03125
- triangles: float32 [3, 512, 512], P(None, None, 'vec'), may hold values from -0.04 to 2, as said below
Outputs:
- transformed: float32 [32768, 2048], P('row', 'vec')
Inputs may be any that keep to these rules, and one draw needn't show every extreme that they name: Each triangles[k] is upper triangular with a diagonal between 0.5 and 2.
All inputs are finite; a program needn't handle non-finite values.
Results may differ from a plain program's by a relative error of at most 0.0001.
Values sent between devices are 32-bit elements; how exact they have to be, the bound alone decides.
A program may use at most 64 MiB of HBM per device.

v0:
```python
import jax
import jax.numpy as jnp
from jax import lax
from jax.sharding import Mesh
from jax.sharding import PartitionSpec as P

VEC = ("vec_0", "vec_1")
ROW_VEC = ("row", "vec_0", "vec_1")


def whole_of(x, axes, dim):
    for axis in reversed(axes):
        x = lax.all_gather(x, axis, axis=dim, tiled=True)
    return x


def cut_along(x, dim, count):
    before, after = (x.shape[:dim], x.shape[dim + 1 :])
    return jnp.moveaxis(x.reshape(*before, count, -1, *after), dim, 0)


def summed_on_arrival(x, axis, dim):
    count = lax.axis_size(axis)
    blocks = lax.all_to_all(cut_along(x, dim, count), axis, 0, 0, tiled=True)
    return jnp.sum(blocks, axis=0)


def from_everyone(x, axis):
    count = lax.axis_size(axis)
    return lax.all_to_all(jnp.broadcast_to(x[None], (count, *x.shape)), axis, 0, 0, tiled=True)


def laid_out(blocks, dim):
    lengths = list(blocks.shape[1:])
    lengths[dim] *= blocks.shape[0]
    return jnp.moveaxis(blocks, 0, dim).reshape(lengths)


def collect(x, axis, dim):
    blocks = from_everyone(x, axis)
    return laid_out(blocks, dim)


def per_device(vectors, reflectors, triangles):
    highest = lax.Precision.HIGHEST
    panels = reflectors.shape[0]
    current = vectors
    sections = lax.all_gather(reflectors, VEC, axis=1, tiled=True)
    factors = whole_of(triangles, VEC, 2)
    for step in range(panels):
        panel = panels - 1 - step
        section = sections[panel]
        factor = factors[panel]
        partial_value = lax.dot_general(
            section,
            current,
            (((0,), (0,)), ((), ())),
            precision=highest,
            preferred_element_type=jnp.float32,
        )
        share = summed_on_arrival(partial_value, "row", 1)
        owned = jnp.dot(factor, share, precision=highest, preferred_element_type=jnp.float32)
        coefficients = collect(owned, "row", 1)
        current = current - jnp.dot(
            section, coefficients, precision=highest, preferred_element_type=jnp.float32
        )
    return current


def solution(mesh):
    finer = Mesh(mesh.devices.reshape(mesh.shape["row"], 4, 4), ("row", "vec_0", "vec_1"))
    placed = (P("row", VEC), P(None, ROW_VEC, None), P(None, None, VEC))
    return jax.shard_map(
        per_device, mesh=finer, in_specs=placed, out_specs=P("row", VEC), check_vma=False
    )
```

profile of v0, /device:TPU:1, one launch (start us, length us, event | category | flops | bytes accessed | tf_op | source)
XLA Modules:
  0.0 311.0 jit_solution(14054268650420613728)
XLA Ops:
  6.5 0.7 all-gather.3.cloned.1.call-update
  7.3 14.0 %all_gather.10 = f32[3,512,128]{1,2,0:T(8,128)} all-gather(f32[3,512,32]{1,2,0:T(8,128)} %param.5), channel_id=1, replica_groups=mesh['row'=32,'vec_0'=4,'vec_1'=4] {'vec_1'}, dimensions={2}, use_global_device_ids=true | all-gather | bytes 983040 | tf_op jit(solution)/shard_map/all_gather | solution.py:13
  21.3 1.2 copy.17
  22.7 69.4 %all-gather.3.cloned.1.call-done = f32[3,1024,512]{2,1,0:T(8,128)} async-done(((f32[3,64,512]{2,1,0:T(8,128)}), f32[3,1024,512]{2,1,0:T(8,128)}) %all-gather.3.cloned.1.call-update) | async-done | bytes 6291472 | tf_op jit(solution)/shard_map/all_gather | solution.py:48
  92.1 3.1 fusion.22
  95.4 35.2 %all_to_all.30 = f32[32,512,4]{1,2,0:T(4,128)S(1)} all-to-all(f32[32,512,4]{1,2,0:T(4,128)S(1)} %copy.19), channel_id=1, replica_groups=mesh['row'=32,'vec_0'=4,'vec_1'=4] {'row'}, dimensions={0} | all-to-all | bytes 524288 | tf_op jit(solution)/shard_map/all_to_all | solution.py:24
  130.7 10.5 %all-gather.5.cloned.1.call-done = f32[3,512,512]{1,2,0:T(8,128)} async-done(((f32[3,512,128]{1,2,0:T(8,128)}), f32[3,512,512]{1,2,0:T(8,128)}) %all-gather.5.cloned.1.call-update) | async-done | bytes 3145744 | tf_op jit(solution)/shard_map/all_gather | solution.py:13
  141.2 1.8 convolution_bitcast_fusion.2
  143.0 0.7 broadcast_in_dim.6
  143.8 13.2 %all-to-all-start.1 = ((f32[32,512,4]{1,2,0:T(4,128)}), f32[32,512,4]{1,2,0:T(4,128)S(1)}, u32[]{:S(2)}, u32[]{:S(2)}) async-start(f32[32,512,4]{1,2,0:T(4,128)} %broadcast_in_dim.6), calls=%async_computation.1 | async-start | bytes 524288 | tf_op jit(solution)/shard_map/all_to_all | solution.py:30
  157.0 0.2 copy.20
  157.2 22.0 %all-to-all-done.1 = f32[32,512,4]{1,2,0:T(4,128)S(1)} async-done(((f32[32,512,4]{1,2,0:T(4,128)}), f32[32,512,4]{1,2,0:T(4,128)S(1)}, u32[]{:S(2)}, u32[]{:S(2)}) %all-to-all-start.1) | async-done | bytes 262176 | tf_op jit(solution)/shard_map/all_to_all | solution.py:30
  179.3 3.9 %fusion.15 = f32[1024,128]{0,1:T(8,128)S(1)} fusion(f32[1024,128]{0,1:T(8,128)S(1)} %copy.20, f32[512,128]{0,1:T(8,128)S(1)} %reshape.20, f32[3,1024,512]{2,1,0:T(8,128)} %all-gather.3.cloned.1.call-done), kind=kOutput, calls=%fused_computation.15 | convolution fusion | flops 805437440 | bytes 3407872 | tf_op jit(solution)/shard_map/dot_general | solution.py:64
  183.2 2.9 fusion.21
  186.1 24.9 %all_to_all.31 = f32[32,512,4]{1,2,0:T(4,128)S(1)} all-to-all(f32[32,512,4]{1,2,0:T(4,128)S(1)} %bitcast.91), channel_id=1, replica_groups=mesh['row'=32,'vec_0'=4,'vec_1'=4] {'row'}, dimensions={0} | all-to-all | bytes 524288 | tf_op jit(solution)/shard_map/all_to_all | solution.py:24
  211.1 1.8 convolution_bitcast_fusion.1
  213.0 25.9 %all_to_all.32 = f32[32,512,4]{1,2,0:T(4,128)S(1)} all-to-all(f32[32,512,4]{1,2,0:T(4,128)S(1)} %broadcast_in_dim.7), channel_id=1, replica_groups=mesh['row'=32,'vec_0'=4,'vec_1'=4] {'row'}, dimensions={0} | all-to-all | bytes 524288 | tf_op jit(solution)/shard_map/all_to_all | solution.py:30
  239.0 3.9 %fusion.18 = f32[1024,128]{0,1:T(8,128)S(1)} fusion(f32[1024,128]{0,1:T(8,128)S(1)} %fusion.15, f32[512,128]{0,1:T(8,128)S(1)} %reshape.22, f32[3,1024,512]{2,1,0:T(8,128)} %all-gather.3.cloned.1.call-done), kind=kOutput, calls=%fused_computation.16 | convolution fusion | flops 805437440 | bytes 3407872 | tf_op jit(solution)/shard_map/dot_general | solution.py:64
  242.9 2.9 fusion.20
  245.8 25.6 %all_to_all.33 = f32[32,512,4]{1,2,0:T(4,128)S(1)} all-to-all(f32[32,512,4]{1,2,0:T(4,128)S(1)} %bitcast.93), channel_id=1, replica_groups=mesh['row'=32,'vec_0'=4,'vec_1'=4] {'row'}, dimensions={0} | all-to-all | bytes 524288 | tf_op jit(solution)/shard_map/all_to_all | solution.py:24
  271.5 1.8 convolution_bitcast_fusion
  273.4 25.8 %all_to_all.34 = f32[32,512,4]{1,2,0:T(4,128)S(1)} all-to-all(f32[32,512,4]{1,2,0:T(4,128)S(1)} %broadcast_in_dim.8), channel_id=1, replica_groups=mesh['row'=32,'vec_0'=4,'vec_1'=4] {'row'}, dimensions={0} | all-to-all | bytes 524288 | tf_op jit(solution)/shard_map/all_to_all | solution.py:30
  299.3 3.9 %fusion.19 = f32[1024,128]{0,1:T(8,128)S(1)} fusion(f32[1024,128]{0,1:T(8,128)S(1)} %fusion.18, f32[512,128]{0,1:T(8,128)S(1)} %reshape.24, f32[3,1024,512]{2,1,0:T(8,128)} %all-gather.3.cloned.1.call-done), kind=kOutput, calls=%fused_computation.17 | convolution fusion | flops 805437440 | bytes 3407872 | tf_op jit(solution)/shard_map/dot_general | solution.py:64
  303.1 1.0 copy.21
  (17 shorter events, 1.1 us)
Async XLA Ops:
  6.5 85.6 %all-gather.3.cloned.1.call-start = ((), (), s32[]{:S(2)}) async-start(), calls=%async_computation.6 | async-start | bytes 6684672 | tf_op jit(solution)/shard_map/all_gather | solution.py:48
  7.3 133.9 %all-gather.5.cloned.1.call-start = ((), (), s32[]{:S(2)}) async-start(), calls=%async_computation.7 | async-start | bytes 3932160 | tf_op jit(solution)/shard_map/all_gather | solution.py:13
  22.7 134.2 %copy-start = (f32[1024,128]{1,0:T(8,128)S(1)}, f32[1024,128]{1,0:T(8,128)}, u32[]{:S(2)}) copy-start(f32[1024,128]{1,0:T(8,128)} %param.3) | copy-start | bytes 1572868
  143.8 35.4 %all-to-all-start.1 = ((f32[32,512,4]{1,2,0:T(4,128)}), f32[32,512,4]{1,2,0:T(4,128)S(1)}, u32[]{:S(2)}, u32[]{:S(2)}) async-start(f32[32,512,4]{1,2,0:T(4,128)} %broadcast_in_dim.6), calls=%async_computation.1 | async-start | bytes 524288 | tf_op jit(solution)/shard_map/all_to_all | solution.py:30
Sparse Core Ops, SparseCore 0:
  10.3 81.6 all-gather.2
  94.2 46.9 all-gather.4
where the time goes:
time: 312 us; the launch traced here: 311 us
  blocking collectives  151 us (48%)
  waiting for transfers between devices  103 us (33%)
  matrix products  25.9 us (8%)
  between operations  13.5 us (4%)
  starting transfers between devices  13.2 us (4%)
  local copies, waits for them, and re-layouts  3.99 us (1%)
    all_to_all x3, blocking collectives, summed_on_arrival(): blocks = lax.all_to_all(cut_along(x, dim, count), axis, 0, 0, tiled=True)  85.8 us
    all_gather x1, waiting for transfers between devices, per_device(): sections = lax.all_gather(reflectors, VEC, axis=1, tiled=True)  69.4 us
    all_to_all x2, blocking collectives, from_everyone(): lax.all_to_all(jnp.broadcast_to(x[None], (count, *x.shape)), axis, 0, 0,...  51.7 us
    all_to_all x1, waiting for transfers between devices, from_everyone(): lax.all_to_all(jnp.broadcast_to(x[None], (count, *x.shape)), axis, 0, 0,...  22 us
    all_gather x1, blocking collectives, whole_of(): x = lax.all_gather(x, axis, axis=dim, tiled=True)  14 us
    all_to_all x1, starting transfers between devices, from_everyone(): lax.all_to_all(jnp.broadcast_to(x[None], (count, *x.shape)), axis, 0, 0,...  13.2 us
    dot_general x3, matrix products, per_device(): jnp.dot(section, coefficients, precision=highest, preferred_element_type=...  11.6 us
    all_gather x1, waiting for transfers between devices, whole_of(): x = lax.all_gather(x, axis, axis=dim, tiled=True)  10.5 us
  transfers between devices with their start and end apart: 3, of which 3 were waited for; matrix products, arithmetic and copies ran while one was open for 2% of the time, Pallas kernels for 0%

commit v1 on v0

--- a/solution.py
+++ b/solution.py
@@ -45,7 +45,9 @@
     highest = lax.Precision.HIGHEST
     panels = reflectors.shape[0]
     current = vectors
-    sections = lax.all_gather(reflectors, VEC, axis=1, tiled=True)
+    sections = jnp.concatenate(
+        lax.all_to_all(jnp.stack([reflectors] * lax.axis_size(VEC)), VEC, 0, 0), axis=1
+    )
     factors = whole_of(triangles, VEC, 2)
     for step in range(panels):
         panel = panels - 1 - step

time: 312 us -> 338 us (1.083)
  blocking collectives: 151 us -> 243 us
  waiting for transfers between devices: 103 us -> 24.5 us
  local copies, waits for them, and re-layouts: 3.99 us -> 14.8 us
  starting transfers between devices: 13.2 us -> 21 us
  matrix products: 25.9 us -> 19.8 us
    all_gather x1, blocking collectives: 14 us -> 94.2 us  [whole_of(): x = lax.all_gather(x, axis, axis=dim, tiled=True)]
    all_gather x1 -> x0, waiting for transfers between devices: 69.4 us -> none  [per_device(): sections = lax.all_gather(reflectors, VEC, axis=1, tiled=True)]
    all_to_all x3, blocking collectives: 85.8 us -> 97.5 us  [summed_on_arrival(): blocks = lax.all_to_all(cut_along(x, dim, count), axis, 0, 0, tiled=True)]
    all_to_all x0 -> x1, starting transfers between devices: none -> 7.75 us  [per_device(): lax.all_to_all(jnp.stack([reflectors] * lax.axis_size(VEC)), VEC, 0, 0)]
    all_gather x1, waiting for transfers between devices: 10.5 us -> 3.17 us  [whole_of(): x = lax.all_gather(x, axis, axis=dim, tiled=True)]
    slice x0 -> x1, local copies, waits for them, and re-layouts: none -> 5.25 us  [per_device(): section = sections[panel]]
    dot_general x3, matrix products: 8.86 us -> 4.12 us  [per_device(): lax.dot_general(section, current, (((0,), (0,)), ((), ())), precision=hig...]
    another operation x0 -> x1, local copies, waits for them, and re-layouts: none -> 4.45 us  [per_device(): jnp.stack([reflectors] * lax.axis_size(VEC))]
  transfers between devices with their start and end apart: 3 -> 3, of which waited for: 3 -> 2; matrix products, arithmetic and copies ran while one was open for 2% -> 2% of each run, Pallas kernels for 0% -> 0%
where the time goes in v1:
time: 338 us; the launch traced here: 337 us
  blocking collectives  243 us (72%)
  waiting for transfers between devices  24.5 us (7%)
  starting transfers between devices  21 us (6%)
  matrix products  19.8 us (6%)
  local copies, waits for them, and re-layouts  14.8 us (4%)
  between operations  13.6 us (4%)
    all_to_all x3, blocking collectives, summed_on_arrival(): blocks = lax.all_to_all(cut_along(x, dim, count), axis, 0, 0, tiled=True)  97.5 us
    all_gather x1, blocking collectives, whole_of(): x = lax.all_gather(x, axis, axis=dim, tiled=True)  94.2 us
    all_to_all x2, blocking collectives, from_everyone(): lax.all_to_all(jnp.broadcast_to(x[None], (count, *x.shape)), axis, 0, 0,...  51.7 us
    all_to_all x1, waiting for transfers between devices, from_everyone(): lax.all_to_all(jnp.broadcast_to(x[None], (count, *x.shape)), axis, 0, 0,...  21.3 us
    all_to_all x1, starting transfers between devices, from_everyone(): lax.all_to_all(jnp.broadcast_to(x[None], (count, *x.shape)), axis, 0, 0,...  13.2 us
    dot_general x3, matrix products, per_device(): jnp.dot(section, coefficients, precision=highest, preferred_element_type=...  10.2 us
    all_to_all x1, starting transfers between devices, per_device(): lax.all_to_all(jnp.stack([reflectors] * lax.axis_size(VEC)), VEC, 0, 0)  7.75 us
  transfers between devices with their start and end apart: 3, of which 2 were waited for; matrix products, arithmetic and copies ran while one was open for 2% of the time, Pallas kernels for 0%

profile of v1, /device:TPU:1, one launch (start us, length us, event | category | flops | bytes accessed | tf_op | source)
XLA Modules:
  0.0 337.3 jit_solution(9733743806230166137)
XLA Ops:
  6.5 4.5 %stack.2 = f32[16,3,64,512]{3,2,1,0:T(8,128)} broadcast(f32[3,64,512]{2,1,0:T(8,128)} %param.4), dimensions={1,2,3} | broadcast | bytes 6684672 | tf_op jit(solution)/shard_map/stack | solution.py:49
  11.0 7.7 %all-to-all-start = ((f32[16,3,64,512]{3,2,1,0:T(8,128)}), f32[16,3,64,512]{3,2,1,0:T(8,128)}, u32[]{:S(2)}, u32[]{:S(2)}) async-start(f32[16,3,64,512]{3,2,1,0:T(8,128)} %stack.2), calls=%async_computation | async-start | bytes 12582912 | tf_op jit(solution)/shard_map/all_to_all | solution.py:49
  18.8 94.2 %all_gather.6 = f32[3,512,128]{1,2,0:T(8,128)} all-gather(f32[3,512,32]{1,2,0:T(8,128)S(1)} %copy-done.3), channel_id=1, replica_groups=mesh['row'=32,'vec_0'=4,'vec_1'=4] {'vec_1'}, dimensions={2}, use_global_device_ids=true | all-gather | bytes 983040 | tf_op jit(solution)/shard_map/all_gather | solution.py:13
  113.5 5.3 %fusion.4 = (f32[1,16,64,512]{3,2,0,1:T(8,128)S(1)}, f32[1,16,64,512]{3,2,0,1:T(8,128)}, f32[1,16,64,512]{3,2,0,1:T(8,128)S(1)}) fusion(f32[3,16,64,512]{3,2,0,1:T(8,128)} %bitcast), kind=kLoop, calls=%fused_computation.16 | loop fusion | bytes 12582912 | tf_op jit(solution)/shard_map/slice | solution.py:54
  118.7 1.4 copy-done.1
  120.1 1.5 convolution_bitcast_fusion.5
  121.8 47.0 %all_to_all.35 = f32[32,512,4]{1,2,0:T(4,128)S(1)} all-to-all(f32[32,512,4]{1,2,0:T(4,128)S(1)} %copy.19), channel_id=1, replica_groups=mesh['row'=32,'vec_0'=4,'vec_1'=4] {'row'}, dimensions={0} | all-to-all | bytes 524288 | tf_op jit(solution)/shard_map/all_to_all | solution.py:24
  168.8 3.2 all-gather.2.cloned.1.call-done
  172.0 1.8 convolution_bitcast_fusion.8
  174.6 13.2 %all-to-all-start.2 = ((f32[32,512,4]{1,2,0:T(4,128)}), f32[32,512,4]{1,2,0:T(4,128)S(1)}, u32[]{:S(2)}, u32[]{:S(2)}) async-start(f32[32,512,4]{1,2,0:T(4,128)} %broadcast_in_dim.6), calls=%async_computation.2 | async-start | bytes 524288 | tf_op jit(solution)/shard_map/all_to_all | solution.py:30
  187.8 1.0 copy.20
  188.8 21.3 %all-to-all-done.2 = f32[32,512,4]{1,2,0:T(4,128)S(1)} async-done(((f32[32,512,4]{1,2,0:T(4,128)}), f32[32,512,4]{1,2,0:T(4,128)S(1)}, u32[]{:S(2)}, u32[]{:S(2)}) %all-to-all-start.2) | async-done | bytes 262176 | tf_op jit(solution)/shard_map/all_to_all | solution.py:30
  210.1 4.1 %fusion = f32[1024,128]{0,1:T(8,128)S(1)} fusion(f32[1024,128]{0,1:T(8,128)} %copy.20, f32[512,128]{0,1:T(8,128)S(1)} %reshape.33, f32[1024,512]{1,0:T(8,128)} %bitcast.74), kind=kOutput, calls=%fused_computation.3 | convolution fusion | flops 805437440 | bytes 3407872 | tf_op jit(solution)/shard_map/dot_general | solution.py:66
  214.2 1.3 convolution_bitcast_fusion.4
  215.6 24.9 %all_to_all.36 = f32[32,512,4]{1,2,0:T(4,128)S(1)} all-to-all(f32[32,512,4]{1,2,0:T(4,128)S(1)} %bitcast.77), channel_id=1, replica_groups=mesh['row'=32,'vec_0'=4,'vec_1'=4] {'row'}, dimensions={0} | all-to-all | bytes 524288 | tf_op jit(solution)/shard_map/all_to_all | solution.py:24
  240.6 1.8 convolution_bitcast_fusion.7
  242.5 25.9 %all_to_all.37 = f32[32,512,4]{1,2,0:T(4,128)S(1)} all-to-all(f32[32,512,4]{1,2,0:T(4,128)S(1)} %broadcast_in_dim.7), channel_id=1, replica_groups=mesh['row'=32,'vec_0'=4,'vec_1'=4] {'row'}, dimensions={0} | all-to-all | bytes 524288 | tf_op jit(solution)/shard_map/all_to_all | solution.py:30
  268.5 3.9 %fusion.1 = f32[1024,128]{0,1:T(8,128)S(1)} fusion(f32[1024,128]{0,1:T(8,128)S(1)} %fusion, f32[512,128]{0,1:T(8,128)S(1)} %reshape.35, f32[1024,512]{1,0:T(8,128)} %bitcast.71), kind=kOutput, calls=%fused_computation.4 | convolution fusion | flops 805437440 | bytes 3407872 | tf_op jit(solution)/shard_map/dot_general | solution.py:66
  272.3 1.3 convolution_bitcast_fusion.3
  273.7 25.6 %all_to_all.38 = f32[32,512,4]{1,2,0:T(4,128)S(1)} all-to-all(f32[32,512,4]{1,2,0:T(4,128)S(1)} %bitcast.79), channel_id=1, replica_groups=mesh['row'=32,'vec_0'=4,'vec_1'=4] {'row'}, dimensions={0} | all-to-all | bytes 524288 | tf_op jit(solution)/shard_map/all_to_all | solution.py:24
  299.4 1.8 convolution_bitcast_fusion.6
  301.3 25.8 %all_to_all.39 = f32[32,512,4]{1,2,0:T(4,128)S(1)} all-to-all(f32[32,512,4]{1,2,0:T(4,128)S(1)} %broadcast_in_dim.8), channel_id=1, replica_groups=mesh['row'=32,'vec_0'=4,'vec_1'=4] {'row'}, dimensions={0} | all-to-all | bytes 524288 | tf_op jit(solution)/shard_map/all_to_all | solution.py:30
  327.1 2.3 fusion.2
  329.4 1.0 copy.21
  (24 shorter events, 2.0 us)
Async XLA Ops:
  11.0 7.8 %copy-start.3 = (f32[3,512,32]{1,2,0:T(8,128)S(1)}, f32[3,512,32]{1,2,0:T(8,128)}, u32[]{:S(2)}) copy-start(f32[3,512,32]{1,2,0:T(8,128)} %param.5) | copy-start | bytes 589828
  11.0 102.5 %all-to-all-start = ((f32[16,3,64,512]{3,2,1,0:T(8,128)}), f32[16,3,64,512]{3,2,1,0:T(8,128)}, u32[]{:S(2)}, u32[]{:S(2)}) async-start(f32[16,3,64,512]{3,2,1,0:T(8,128)} %stack.2), calls=%async_computation | async-start | bytes 12582912 | tf_op jit(solution)/shard_map/all_to_all | solution.py:49
  18.7 94.3 %copy-start.2 = (f32[1024,128]{1,0:T(8,128)S(1)}, f32[1024,128]{1,0:T(8,128)}, u32[]{:S(2)}) copy-start(f32[1024,128]{1,0:T(8,128)} %param.3) | copy-start | bytes 1572868
  18.8 153.2 %all-gather.2.cloned.1.call-start = ((), (), s32[]{:S(2)}) async-start(), calls=%async_computation.7 | async-start | bytes 3932160 | tf_op jit(solution)/shard_map/all_gather | solution.py:13
  118.7 1.4 copy-start.1
  174.6 35.4 %all-to-all-start.2 = ((f32[32,512,4]{1,2,0:T(4,128)}), f32[32,512,4]{1,2,0:T(4,128)S(1)}, u32[]{:S(2)}, u32[]{:S(2)}) async-start(f32[32,512,4]{1,2,0:T(4,128)} %broadcast_in_dim.6), calls=%async_computation.2 | async-start | bytes 524288 | tf_op jit(solution)/shard_map/all_to_all | solution.py:30
  210.1 4.1 %copy-start = (f32[1,16,64,512]{3,2,0,1:T(8,128)S(1)}, f32[1,16,64,512]{3,2,0,1:T(8,128)}, u32[]{:S(2)}) copy-start(f32[1,16,64,512]{3,2,0,1:T(8,128)} %get-tuple-element.6) | copy-start | bytes 6291460
Sparse Core Ops, SparseCore 0:
  113.2 58.7 all-gather.1
